TPU v7x, 32 devices: a whole 2x2x4 slice. The times are simulated.
32 devices in a mesh: member: 4 (over y, core), mesh: 8 (over z, x).
Axes of the slice: x: 2, y: 2, z: 4, core: 2. Of those that a mesh axis runs over, the one named last changes fastest.
Arguments:
- hidden_embedding: bfloat16 [8, 4096, 512], P('member', 'mesh'), may hold values from -6 to 6
- decoder_matrix: bfloat16 [512, 96], replicated, may hold values from -0.25 to 0.25
- baseline_field: float32 [96, 4096], P(None, 'mesh'), may hold values from -6 to 6
- truth_field: float32 [96, 4096], P(None, 'mesh'), may hold values from -6 to 6
- cell_surface_share: float32 [4096], P('mesh'), may hold values from 0.3 to 3
- node_order: int32 [8, 512], P('mesh'), may hold values from 0 to 511, each once within a row
- query: bfloat16 [8, 4096, 512], P('member', 'mesh'), may hold values from -6 to 6
- key_rows: bfloat16 [8, 4096, 512], P('member', 'mesh'), may hold values from -6 to 6
- value_rows: bfloat16 [8, 4096, 512], P('member', 'mesh'), may hold values from -6 to 6
- row_lse: float32 [8, 8, 4096], P('member', None, 'mesh'), may hold values from 6.5 to 8.5
- kv_owner: int32 [8, 8], replicated, may hold values from 0 to 7, each once within a row
- kv_local: int32 [8, 8], replicated, may hold values from 0 to 3
Outputs:
- grad_query: float32 [8, 4096, 512], P('member', 'mesh')
- grad_key: float32 [8, 4096, 512], P('member', 'mesh')
- grad_value: float32 [8, 4096, 512], P('member', 'mesh')
Inputs may be any that keep to these rules, and one draw needn't show every extreme that they name: `kv_owner`: each row names every shard once. `node_order`: each row holds every number of 0 to 511 once.
All inputs are finite; a program needn't handle non-finite values.
Results may differ from a plain program's by a relative error of at most 0.0068.
Values may be sent and summed in bfloat16 or wider, within the bound.
A program may use at most 128 MiB of HBM per device.

v0:
```python
import functools

import jax
import jax.numpy as jnp
from jax import lax
from jax.experimental import pallas as pl
from jax.experimental.pallas import tpu as pltpu
from jax.sharding import PartitionSpec as P

KB = 128
LOSS_SCALE = 4096.0
FAIR_EPS = 0.05
NORM_EPS = 1e-06
MESH = pl.DeviceIdType.MESH

NN = (((1,), (0,)), ((), ()))
NT = (((1,), (1,)), ((), ()))
TN = (((0,), (0,)), ((), ()))


def dot(a, b, dims):
    return lax.dot_general(a, b, dims, preferred_element_type=jnp.float32)


def unit(d):
    return d * lax.rsqrt(jnp.sum(d * d, axis=0, keepdims=True) + NORM_EPS)


def listed_block(me, owner_ref, local_ref, s):
    found = jnp.int32(0)
    for j in range(owner_ref.shape[1]):
        found = jnp.where(owner_ref[s, j] == me, local_ref[s, j], found)
    return found


def columns_of(n):
    cols = 1
    while (2 * cols) ** 2 <= n and n % (2 * cols) == 0:
        cols *= 2
    return cols


def fused_kernel(
    groups,
    C,
    R,
    heads,
    owner_ref,
    local_ref,
    hid_in,
    dec_in,
    dect_in,
    base_in,
    truth_in,
    share_in,
    order_in,
    q_in,
    k_in,
    v_in,
    lse_in,
    contrib,
    own_dq,
    hid,
    dec,
    dect,
    base,
    truth,
    share,
    order,
    lse,
    k_vm,
    v_vm,
    fc,
    select,
    saved,
    deriv,
    cols,
    terms,
    q_buf,
    pick_buf,
    kv_buf,
    kvg,
    dqs,
    dqr,
    dq_in,
    grads,
    total,
    ld_sem,
    f_snd,
    f_rcv,
    q_snd,
    q_rcv,
    c_snd,
    c_rcv,
    kv_snd,
    kv_rcv,
    g_snd,
    g_rcv,
    d_snd,
    d_rcv,
):
    D = R // 2
    E = R - 1 - D
    n = R * C
    members, _, rows, width = q_buf.shape
    chans = base.shape[0]
    dim = width // heads
    pair = 2 * dim
    scale = dim ** (-0.5)
    kb = KB
    me = lax.axis_index("mesh")
    grp = lax.axis_index("member")
    r = lax.div(me, C)
    c = lax.rem(me, C)

    def dev(row, col):
        return {"mesh": row * C + col}

    def remote(src, dst, snd, rcv, device):
        return pltpu.make_async_remote_copy(
            src_ref=src, dst_ref=dst, send_sem=snd, recv_sem=rcv, device_id=device, device_id_type=MESH
        )

    loads = [
        (k_in, k_vm),
        (v_in, v_vm),
        (q_in, None),
        (hid_in, hid),
        (dect_in, dect),
        (base_in, base),
        (dec_in, dec),
        (order_in, order),
        (truth_in, truth),
        (share_in, share),
        (lse_in, lse),
    ]

    def load(i):
        src, dst = loads[i]
        if dst is None:
            dst = q_buf.at[:, r]
        return pltpu.make_async_copy(src, dst, ld_sem.at[i])

    for i in (2, 0, 1, 3, 4, 5, 6, 7, 8, 9, 10):
        load(i).start()

    barrier = pltpu.get_barrier_semaphore()
    reach = max(1, E)
    count = jnp.int32(groups - 1)
    for k in range(1, groups):
        pl.semaphore_signal(
            barrier, inc=1, device_id={"member": lax.rem(grp + k, groups)}, device_id_type=MESH
        )
    for off in range(-reach, reach + 1):
        row = r + off
        ok = (row >= 0) & (row < R)
        for k in range(C):
            if off == 0 and k == 0:
                continue
            col = lax.rem(c + k, C)

            @pl.when(ok)
            def _():
                pl.semaphore_signal(barrier, inc=1, device_id=dev(row, col), device_id_type=MESH)

            count = count + jnp.where(ok, 1, 0)
    pl.semaphore_wait(barrier, count)

    def q_copy(m, q, up):
        return remote(
            q_buf.at[m, q],
            q_buf.at[m, q],
            q_snd.at[m, up, q],
            q_rcv.at[m, q],
            dev(r + (1 if up else -1), c),
        )

    def c_copy(q, up, part):
        ref = (cols, terms)[part]
        return remote(
            ref.at[q], ref.at[q], c_snd.at[part, up, q], c_rcv.at[part, q], dev(r + (1 if up else -1), c)
        )

    def passes(up, h):
        if up:
            return r - h, (r - h >= 0) & (r + 1 < R)
        return r + h, (r + h < R) & (r - 1 >= 0)

    def send_q(m, h):
        for up in (1, 0):
            q, ok = passes(up, h)

            @pl.when(ok)
            def _():
                if h > 0:
                    q_copy(m, q, up).wait_recv()
                q_copy(m, q, up).start()

    def send_c(h):
        for up in (1, 0):
            q, ok = passes(up, h)

            @pl.when(ok)
            def _():
                for part in range(2):
                    if h > 0:
                        c_copy(q, up, part).wait_recv()
                    c_copy(q, up, part).start()

    def host_of(s):
        q = lax.div(s, C)
        col = lax.rem(s, C)
        far = jnp.abs(q - r) > D
        row = jnp.where(far, jnp.where(q > r, q - D, q + D), r)
        slot = jnp.where(far, R * C + (jnp.abs(row - r) - 1) * C + c, q * C + c)
        return row, col, slot, (row == r) & (col == c)

    def kv_copy(m, s):
        row, col, slot, _ = host_of(s)
        return remote(
            pick_buf.at[m, s], kv_buf.at[m, slot], kv_snd.at[m, s], kv_rcv.at[m, slot], dev(row, col)
        )

    load(2).wait()
    send_q(0, 0)
    load(0).wait()
    load(1).wait()

    def pick(i, carry):
        m = lax.div(i, n)
        s = lax.rem(i, n)
        block = listed_block(me, owner_ref, local_ref, s)
        _, _, slot, mine = host_of(s)
        key = k_vm[m, block]
        value = v_vm[m, block]

        @pl.when(mine)
        def _():
            kv_buf[m, slot, 0] = key
            kv_buf[m, slot, 1] = value

        @pl.when(jnp.logical_not(mine))
        def _():
            pick_buf[m, s, 0] = key
            pick_buf[m, s, 1] = value

        return carry

    lax.fori_loop(0, members * n, pick, 0)

    def send_kv(i, carry):
        m = lax.div(i, n)
        s = lax.rem(i, n)

        @pl.when(jnp.logical_not(host_of(s)[3]))
        def _():
            kv_copy(m, s).start()

        return carry

    for i in (3, 4, 5):
        load(i).wait()
    for m in range(members):
        fc[grp, m] = base[...] + dot(dect[...], hid[m], NT)
    lax.fori_loop(0, members * n, send_kv, 0)
    mate = grp + 1 - 2 * lax.rem(grp, 2)

    def f_copy(src, sem, to):
        return remote(fc.at[src], fc.at[src], f_snd.at[sem], f_rcv.at[src], {"member": to})

    cousins = range(1, groups // 2)
    for k in cousins:
        f_copy(grp, k, lax.rem(grp + 2 * k, groups)).start()
    f_copy(grp, 0, mate).start()

    for i in range(6, 11):
        load(i).wait()
    select[...] = (
        lax.broadcasted_iota(jnp.int32, (rows, rows), 0) == order[...]
    ).astype(jnp.bfloat16)
    for m in range(members):
        saved[m] = dot(hid[m], select[...], TN).astype(jnp.bfloat16)
        terms[r, m, pl.ds(0, heads)] = lse[m]

    for h in range(1, D):
        send_q(0, h)
    for k in cousins:
        src = lax.rem(grp + 2 * k, groups)
        f_copy(src, 0, mate).wait_recv()
        f_copy(src, groups // 2 + k, mate).start()
    for k in range(groups // 2):
        f_copy(lax.rem(mate + 2 * k, groups), 0, mate).wait_recv()

    everyone = members * groups
    lanes_step = 128

    def score(i, carry):
        lanes = pl.ds(pl.multiple_of(i * lanes_step, lanes_step), lanes_step)
        weight = LOSS_SCALE * share[:, lanes]
        for m in range(members):
            own = fc[grp, m, :, lanes]
            couple = jnp.zeros_like(own)
            for other in range(groups):
                for k in range(members):
                    couple = couple + unit(own - fc[other, k, :, lanes])
            polarity = unit(own - truth[:, lanes])
            deriv[m, :, lanes] = (
                weight
                * (polarity / everyone - (1.0 - FAIR_EPS) / (everyone * (everyone - 1)) * couple)
            ).astype(jnp.bfloat16)
        return carry

    lax.fori_loop(0, rows // lanes_step, score, 0)

    def latent(m, column):
        grads[...] = dot(dec[...], column, NN).astype(jnp.bfloat16)

    for m in range(members):
        column = dot(deriv[m], select[...], NN).astype(jnp.bfloat16)
        cols[r, m] = column
        latent(m, column)
        for h in range(heads):
            part = pl.ds(h * dim, dim)
            terms[r, m, pl.ds(heads + h, 1)] = jnp.sum(
                grads[part].astype(jnp.float32) * saved[m, part].astype(jnp.float32),
                axis=0,
                keepdims=True,
            )
    send_c(0)
    for m in range(1, members):
        send_q(m, 0)
    for h in range(1, D):
        send_c(h)

    low = lax.broadcasted_iota(jnp.int32, (kb, pair), 1) < dim

    def tile(m, q, slot):
        for p in range(heads // 2):
            lanes = pl.ds(p * pair, pair)
            key = kv_buf[m, slot, 0, :, lanes]
            value = kv_buf[m, slot, 1, :, lanes]
            nought = jnp.zeros_like(key)
            keys = jnp.concatenate(
                [jnp.where(low, key, nought), jnp.where(low, nought, key)], axis=0
            )
            values = jnp.concatenate(
                [jnp.where(low, value, nought), jnp.where(low, nought, value)], axis=0
            )
            q_pair = q_buf[m, q, :, lanes]
            g_pair = grads[lanes, :]
            scores = dot(keys, q_pair, NT)
            dprobs = dot(values, g_pair, NN)
            prob, dscore = [], []
            for k in range(2):
                part = slice(k * kb, (k + 1) * kb)
                h = 2 * p + k
                pr = jnp.exp(scores[part] * scale - terms[q, m, pl.ds(h, 1), :])
                prob.append(pr.astype(jnp.bfloat16))
                dscore.append(
                    (pr * (dprobs[part] - terms[q, m, pl.ds(heads + h, 1), :])).astype(jnp.bfloat16)
                )
            prob = jnp.concatenate(prob, axis=0)
            dscore = jnp.concatenate(dscore, axis=0)
            dv = dot(prob, g_pair, NT)
            dk = dot(dscore, q_pair, NN) * scale
            kvg[m, slot, 0, :, lanes] = jnp.where(low, dk[:kb], dk[kb:]).astype(jnp.bfloat16)
            kvg[m, slot, 1, :, lanes] = jnp.where(low, dv[:kb], dv[kb:]).astype(jnp.bfloat16)
            total[lanes, :] += dot(keys, dscore, TN)

    def tile_place(q, t):
        below = q > r
        turn = lax.div(t, C)
        row = jnp.where(below, r - turn, r + turn)
        slot = jnp.where(turn == 0, q * C + t, R * C + t - C)
        return row, lax.rem(t, C), slot, t == c

    def tile_count(q):
        extra = jnp.where(q == r + D, r, jnp.where(q == r - D, R - 1 - r, 0))
        return C * (1 + extra)

    def g_copy(m, q, t):
        row, col, slot, _ = tile_place(q, t)
        return remote(
            kvg.at[m, slot],
            contrib.at[m, q * C + c],
            g_snd.at[m, slot],
            g_rcv.at[m, q * C + c],
            dev(row, col),
        )

    def g_local(m, q, t):
        _, _, slot, _ = tile_place(q, t)
        return pltpu.make_async_copy(
            kvg.at[m, slot], contrib.at[m, q * C + c], g_rcv.at[m, q * C + c]
        )

    def kv_arrival(m, slot):
        return remote(
            pick_buf.at[0, 0], kv_buf.at[m, slot], kv_snd.at[0, 0], kv_rcv.at[m, slot], dev(r, c)
        )

    def d_copy(m, q, up, last):
        if last:
            dst, sem = dq_in.at[m, 1 - up], d_rcv.at[m, R + 1 - up]
        else:
            dst, sem = dqr.at[m, q], d_rcv.at[m, q]
        return remote(dqs.at[m, q], dst, d_snd.at[m, q], sem, dev(r + (1 if up else -1), c))

    def order_of(step):
        dist = D - lax.div(step, 2)
        q = jnp.where(lax.rem(step, 2) == 0, r + dist, r - dist)
        return q, dist, (q >= 0) & (q < R)

    def job(i, carry):
        m = lax.div(i, 2 * D + 1)
        step = lax.rem(i, 2 * D + 1)
        q, dist, ok = order_of(step)

        @pl.when((step == 2 * D) & (m + 1 < members))
        def _():
            for h in range(1, D):
                send_q(m + 1, h)

        @pl.when(ok)
        def _():
            for up in (1, 0):
                edge = (r == R - 1) if up else (r == 0)
                here = ((q < r) if up else (q > r)) & ((dist == D) | edge)

                @pl.when(here)
                def _():
                    q_copy(m, q, up).wait_recv()

                    @pl.when(m == 0)
                    def _():
                        c_copy(q, up, 0).wait_recv()
                        c_copy(q, up, 1).wait_recv()

            latent(m, cols[q, m])
            total[...] = jnp.zeros_like(total)

            def one(t, carry):
                _, _, slot, mine = tile_place(q, t)

                @pl.when(jnp.logical_not(mine))
                def _():
                    kv_arrival(m, slot).wait_recv()

                tile(m, q, slot)

                @pl.when(mine)
                def _():
                    g_local(m, q, t).start()

                @pl.when(jnp.logical_not(mine))
                def _():
                    g_copy(m, q, t).start()

                return carry

            lax.fori_loop(0, tile_count(q), one, 0)

            @pl.when(dist == 0)
            def _():
                own_dq[m] = total[...] * scale

            for up in (1, 0):
                side = (q > r) if up else (q < r)
                chained = (dist < D) & ((r > 0) if up else (r < R - 1))

                @pl.when(side & chained)
                def _():
                    d_copy(m, q, up, False).wait_recv()
                    dqs[m, q] = (total[...] * scale + dqr[m, q].astype(jnp.float32)).astype(
                        jnp.bfloat16
                    )

                @pl.when(side & jnp.logical_not(chained))
                def _():
                    dqs[m, q] = (total[...] * scale).astype(jnp.bfloat16)

                @pl.when(side & (dist == 1))
                def _():
                    d_copy(m, q, up, True).start()

                @pl.when(side & (dist > 1))
                def _():
                    d_copy(m, q, up, False).start()

        return carry

    lax.fori_loop(0, members * (2 * D + 1), job, 0)

    for m in range(members):
        for up in (1, 0):
            @pl.when((r > 0) if up else (r < R - 1))
            def _():
                d_copy(m, r, up, True).wait_recv()
                own_dq[m] = own_dq[m] + dq_in[m, 1 - up].astype(jnp.float32)

    def last(i, carry):
        m = lax.div(i, n)
        s = lax.rem(i, n)
        pltpu.make_async_copy(kvg.at[0, 0], contrib.at[m, s], g_rcv.at[m, s]).wait()

        @pl.when(jnp.logical_not(host_of(s)[3]))
        def _():
            kv_copy(m, s).wait_send()

        return carry

    lax.fori_loop(0, members * n, last, 0)

    def sent(i, carry):
        m = lax.div(i, 2 * D + 1)
        q, dist, ok = order_of(lax.rem(i, 2 * D + 1))

        @pl.when(ok)
        def _():
            def one(t, carry):
                @pl.when(jnp.logical_not(tile_place(q, t)[3]))
                def _():
                    g_copy(m, q, t).wait_send()

                return carry

            lax.fori_loop(0, tile_count(q), one, 0)

            @pl.when(dist > 0)
            def _():
                d_copy(m, q, 1, False).wait_send()

        return carry

    lax.fori_loop(0, members * (2 * D + 1), sent, 0)
    for h in range(D):
        for up in (1, 0):
            q, ok = passes(up, h)

            @pl.when(ok)
            def _():
                for m in range(members):
                    q_copy(m, q, up).wait_send()
                for part in range(2):
                    c_copy(q, up, part).wait_send()

    f_copy(grp, 0, mate).wait_send()
    for k in cousins:
        f_copy(grp, k, mate).wait_send()
        f_copy(grp, groups // 2 + k, mate).wait_send()


def fused(groups, n, heads, blocks, arrays):
    (_, _, hid, dec, dect, base, truth, share, order, q, k, v, lse) = arrays
    C = columns_of(n)
    R = n // C
    D = R // 2
    E = R - 1 - D
    members, rows, width = hid.shape
    chans = base.shape[0]
    bf, f32 = jnp.bfloat16, jnp.float32
    slots = (R + E) * C
    vm = pltpu.VMEM
    dma = pltpu.SemaphoreType.DMA
    scratch = [
        vm(hid.shape, bf),
        vm(dec.shape, bf),
        vm(dect.shape, bf),
        vm(base.shape, f32),
        vm(truth.shape, f32),
        vm(share.shape, f32),
        vm(order.shape, jnp.int32),
        vm(lse.shape, f32),
        vm(k.shape, bf),
        vm(v.shape, bf),
        vm((groups, members, chans, rows), f32),
        vm((rows, rows), bf),
        vm((members, width, rows), bf),
        vm((members, chans, rows), bf),
        vm((R, members, chans, rows), bf),
        vm((R, members, 2 * heads, rows), f32),
        vm((members, R, rows, width), bf),
        vm((members, n, 2, KB, width), bf),
        vm((members, slots, 2, KB, width), bf),
        vm((members, slots, 2, KB, width), bf),
        vm((members, R, width, rows), bf),
        vm((members, R, width, rows), bf),
        vm((members, 2, width, rows), bf),
        vm((width, rows), bf),
        vm((width, rows), f32),
        dma((11,)),
        dma((groups,)),
        dma((groups,)),
        dma((members, 2, R)),
        dma((members, R)),
        dma((2, 2, R)),
        dma((2, R)),
        dma((members, n)),
        dma((members, slots)),
        dma((members, slots)),
        dma((members, n)),
        dma((members, R)),
        dma((members, R + 2)),
    ]
    smem = pl.BlockSpec(memory_space=pltpu.SMEM)
    anyw = pl.BlockSpec(memory_space=pl.ANY)
    tiles = members * n
    return pl.pallas_call(
        functools.partial(fused_kernel, groups, C, R, heads),
        out_shape=[
            jax.ShapeDtypeStruct((members, n, 2, KB, width), bf),
            jax.ShapeDtypeStruct((members, width, rows), f32),
        ],
        in_specs=[smem, smem] + [anyw] * 11,
        out_specs=[anyw, pl.BlockSpec(memory_space=pltpu.VMEM)],
        scratch_shapes=scratch,
        compiler_params=pltpu.CompilerParams(
            collective_id=0, has_side_effects=True, vmem_limit_bytes=60 * 2**20
        ),
        cost_estimate=pl.CostEstimate(
            flops=tiles * 10 * rows * KB * width,
            bytes_accessed=16 * 2**20,
            transcendentals=tiles * heads * rows * KB,
        ),
        name="fused",
    )(*arrays)


def collect_kernel(me_ref, owner_ref, local_ref, contrib, own_dq, gq, gk, gv):
    gq[0] = own_dq[0].T
    gk[...] = jnp.zeros_like(gk)
    gv[...] = jnp.zeros_like(gv)
    for s in range(contrib.shape[1]):
        block = listed_block(me_ref[0], owner_ref, local_ref, s)
        gk[0, block] += contrib[0, s, 0].astype(jnp.float32)
        gv[0, block] += contrib[0, s, 1].astype(jnp.float32)


def collect(blocks, tables, contrib, own_dq):
    members, n, _, kb, width = contrib.shape
    rows = own_dq.shape[2]
    steps = 4
    kv_shape = jax.ShapeDtypeStruct((members, blocks, kb, width), jnp.float32)
    kv_spec = pl.BlockSpec((1, blocks, kb // steps, width), lambda m, i, *_: (m, 0, i, 0))
    return pl.pallas_call(
        collect_kernel,
        out_shape=[jax.ShapeDtypeStruct((members, rows, width), jnp.float32), kv_shape, kv_shape],
        grid_spec=pltpu.PrefetchScalarGridSpec(
            num_scalar_prefetch=3,
            grid=(members, steps),
            in_specs=[
                pl.BlockSpec((1, n, 2, kb // steps, width), lambda m, i, *_: (m, 0, 0, i, 0)),
                pl.BlockSpec((1, width, rows // steps), lambda m, i, *_: (m, 0, i)),
            ],
            out_specs=[
                pl.BlockSpec((1, rows // steps, width), lambda m, i, *_: (m, i, 0)),
                kv_spec,
                kv_spec,
            ],
        ),
        compiler_params=pltpu.CompilerParams(vmem_limit_bytes=24 * 2**20),
        cost_estimate=pl.CostEstimate(flops=10**6, bytes_accessed=12 * 2**20, transcendentals=0),
        name="collect",
    )(*tables, contrib, own_dq)


def shards(
    groups,
    n,
    hidden_embedding,
    decoder_matrix,
    baseline_field,
    truth_field,
    cell_surface_share,
    node_order,
    query,
    key_rows,
    value_rows,
    row_lse,
    kv_owner,
    kv_local,
):
    members, nodes, width = hidden_embedding.shape
    heads = row_lse.shape[1]
    blocks = nodes // KB
    split = (members, blocks, KB, width)
    contrib, own_dq = fused(
        groups,
        n,
        heads,
        blocks,
        (
            kv_owner,
            kv_local,
            hidden_embedding,
            decoder_matrix,
            decoder_matrix.T,
            baseline_field,
            truth_field,
            cell_surface_share[None],
            node_order,
            query,
            key_rows.reshape(split),
            value_rows.reshape(split),
            row_lse,
        ),
    )
    me = jnp.full((1,), lax.axis_index("mesh"), jnp.int32)
    gq, gk, gv = collect(blocks, (me, kv_owner, kv_local), contrib, own_dq)
    return gq, gk.reshape(key_rows.shape), gv.reshape(value_rows.shape)


def solution(mesh):
    rows = P("member", "mesh", None)
    return jax.shard_map(
        functools.partial(shards, mesh.shape["member"], mesh.shape["mesh"]),
        mesh=mesh,
        in_specs=(
            rows,
            P(),
            P(None, "mesh"),
            P(None, "mesh"),
            P("mesh"),
            P("mesh", None),
            rows,
            rows,
            rows,
            P("member", None, "mesh"),
            P(),
            P(),
        ),
        out_specs=(rows, rows, rows),
        check_vma=False,
    )
```

profile of v0, /device:TPU:10, one launch (start us, length us, event | category | flops | bytes accessed | tf_op | source)
XLA Modules:
  0.0 143.5 jit_solution(7688897224322320332)
XLA Ops:
  0.6 1.7 %copy.15.dec_in = bf16[512,96]{1,0:T(8,128)(2,1)} copy(bf16[512,96]{0,1:T(8,128)(2,1)} %param.13) | data formatting | bytes 196608 | tf_op args[1]
  2.3 0.0 copy-start.2
  2.3 0.0 copy-start.3
  2.3 132.0 %fused.1 = (bf16[2,8,2,128,512]{4,3,2,1,0:T(8,128)(2,1)}, f32[2,512,512]{2,1,0:T(8,128)}) custom-call(s32[8,8]{1,0:T(8,128)} %owner_ref.3, s32[8,8]{1,0:T(8,128)} %local_ref.3, bf16[2,512,512]{2,1,0:T(8,128)(2,1)} %hid_in.1, bf16[512,96]{1,0:T(8,128)(2,1)} %copy.15.dec_in, bf16[96,512]{1,0:T(8,128)(2,1)} %bitcast.7, f32[96,512]{1,0:T(8,128)} %base_in.1, ...), custom_call_target="tpu_custom_call" | custom-call | flops 5368709120 | bytes 16777216 | tf_op jit(solution)/shard_map/fused/pallas_call | solution.py:608
  134.3 0.0 copy-done.2
  134.3 0.0 copy-done.3
  134.3 0.0 copy-start
  134.3 2.2 %copy-done = bf16[2,8,2,128,512]{4,3,2,1,0:T(8,128)(2,1)S(1)} copy-done((bf16[2,8,2,128,512]{4,3,2,1,0:T(8,128)(2,1)S(1)}, bf16[2,8,2,128,512]{4,3,2,1,0:T(8,128)(2,1)}, u32[]{:S(2)}) %copy-start) | copy-done | bytes 4194328
  136.5 0.0 copy-start.1
  136.5 1.6 %copy-done.1 = f32[2,512,512]{2,1,0:T(8,128)S(1)} copy-done((f32[2,512,512]{2,1,0:T(8,128)S(1)}, f32[2,512,512]{2,1,0:T(8,128)}, u32[]{:S(2)}) %copy-start.1) | copy-done | bytes 2097176
  138.1 5.4 %collect.1 = (f32[2,512,512]{2,1,0:T(8,128)}, f32[2,4,128,512]{3,2,1,0:T(8,128)}, f32[2,4,128,512]{3,2,1,0:T(8,128)}) custom-call(s32[1]{0:T(128)} %bitcast.me_ref, s32[8,8]{1,0:T(8,128)S(1)} %copy-done.2, s32[8,8]{1,0:T(8,128)S(1)} %copy-done.3, bf16[2,8,2,128,512]{4,3,2,1,0:T(8,128)(2,1)S(1)} %copy-done, f32[2,512,512]{2,1,0:T(8,128)S(1)} %copy-done.1), custom_call_target="tpu_custom_call" | custom-call | flops 1000000 | bytes 12582912 | tf_op jit(solution)/shard_map/collect/pallas_call | solution.py:645
Async XLA Ops:
  2.3 132.0 %copy-start.2 = (s32[8,8]{1,0:T(8,128)S(1)}, s32[8,8]{1,0:T(8,128)}, u32[]{:S(2)}) copy-start(s32[8,8]{1,0:T(8,128)} %owner_ref.3) | copy-start | bytes 772
  2.3 132.0 %copy-start.3 = (s32[8,8]{1,0:T(8,128)S(1)}, s32[8,8]{1,0:T(8,128)}, u32[]{:S(2)}) copy-start(s32[8,8]{1,0:T(8,128)} %local_ref.3) | copy-start | bytes 772
  134.3 2.2 %copy-start = (bf16[2,8,2,128,512]{4,3,2,1,0:T(8,128)(2,1)S(1)}, bf16[2,8,2,128,512]{4,3,2,1,0:T(8,128)(2,1)}, u32[]{:S(2)}) copy-start(bf16[2,8,2,128,512]{4,3,2,1,0:T(8,128)(2,1)} %get-tuple-element.8.contrib) | copy-start | bytes 12582916
  136.5 1.6 %copy-start.1 = (f32[2,512,512]{2,1,0:T(8,128)S(1)}, f32[2,512,512]{2,1,0:T(8,128)}, u32[]{:S(2)}) copy-start(f32[2,512,512]{2,1,0:T(8,128)} %get-tuple-element.9.own_dq) | copy-start | bytes 6291460
where the time goes:
time: 144 us
  Pallas kernels  137 us (95%)
  local copies, waits for them, and re-layouts  5.43 us (4%)
    pallas_call x1, Pallas kernels, fused(): pl.pallas_call(functools.partial(fused_kernel, groups, C, R, heads), out_...  132 us
    unnamed x9, local copies, waits for them, and re-layouts  5.43 us
    pallas_call x1, Pallas kernels, collect(): pl.pallas_call(collect_kernel, out_shape=[jax.ShapeDtypeStruct((members,...  5.4 us

commit v1 on v0

v1 whole, which is shorter than its diff:
```python
import functools
import math

import jax
import jax.numpy as jnp
from jax import lax
from jax.experimental import pallas as pl
from jax.experimental.pallas import tpu as pltpu
from jax.sharding import PartitionSpec as P

KB = 128
LOSS_SCALE = 4096.0
FAIR_EPS = 0.05
NORM_EPS = 1e-06
PIECES = 2
VMEM_LIMIT = 63 * 2**20
VMEM_SPARE = 2 * 2**20
VMEM_GAP = 2**19
MESH = pl.DeviceIdType.MESH

NN = (((1,), (0,)), ((), ()))
NT = (((1,), (1,)), ((), ()))
TN = (((0,), (0,)), ((), ()))


def dot(a, b, dims):
    return lax.dot_general(a, b, dims, preferred_element_type=jnp.float32)


def unit(d):
    return d * lax.rsqrt(jnp.sum(d * d, axis=0, keepdims=True) + NORM_EPS)


def listed_block(me, owner_ref, local_ref, s):
    found = jnp.int32(0)
    for j in range(owner_ref.shape[1]):
        found = jnp.where(owner_ref[s, j] == me, local_ref[s, j], found)
    return found


def columns_of(n):
    cols = 1
    while (2 * cols) ** 2 <= n and n % (2 * cols) == 0:
        cols *= 2
    return cols


def fused_kernel(
    groups,
    C,
    R,
    heads,
    near,
    owner_ref,
    local_ref,
    hid_in,
    dect_in,
    base_in,
    truth_in,
    share_in,
    order_in,
    q_in,
    k_in,
    v_in,
    lse_in,
    gq_out,
    gk_out,
    gv_out,
    land,
    hid,
    dect,
    base,
    truth,
    share,
    order,
    lse,
    k_vm,
    v_vm,
    fc,
    select,
    deriv,
    cols,
    terms,
    q_buf,
    pick_buf,
    kv_buf,
    kvg,
    kv_sum,
    dq_sum,
    acc,
    part,
    dqs,
    dqr,
    dq_in,
    grads,
    total,
    ld_sem,
    f_snd,
    f_rcv,
    q_snd,
    q_rcv,
    c_snd,
    c_rcv,
    kv_snd,
    kv_rcv,
    g_snd,
    g_rcv,
    d_snd,
    d_rcv,
    l_rcv,
    o_sem,
    stage,
):
    D = R // 2
    E = R - 1 - D
    n = R * C
    members, _, rows, width = q_buf.shape
    dim = width // heads
    pair = 2 * dim
    scale = dim ** (-0.5)
    kb = KB
    me = lax.axis_index("mesh")
    grp = lax.axis_index("member")
    r = lax.div(me, C)
    c = lax.rem(me, C)
    mate = grp + 1 - 2 * lax.rem(grp, 2)
    cousins = range(1, groups // 2)

    def dev(row, col):
        return {"mesh": row * C + col}

    def remote(src, dst, snd, rcv, device):
        return pltpu.make_async_remote_copy(
            src_ref=src, dst_ref=dst, send_sem=snd, recv_sem=rcv, device_id=device, device_id_type=MESH
        )

    loads = [
        (q_in, None),
        (hid_in, hid),
        (dect_in, dect),
        (base_in, base),
        (k_in, k_vm),
        (v_in, v_vm),
        (order_in, order),
        (truth_in, truth),
        (share_in, share),
        (lse_in, lse),
    ]

    def load(i):
        src, dst = loads[i]
        if dst is None:
            dst = q_buf.at[:, r]
        return pltpu.make_async_copy(src, dst, ld_sem.at[i])

    barrier = pltpu.get_barrier_semaphore()

    def greet(device):
        pl.semaphore_signal(barrier, inc=1, device_id=device, device_id_type=MESH)

    greet({"member": mate})
    for k in cousins:
        greet({"member": lax.rem(grp + 2 * k, groups)})
    count = jnp.int32(groups // 2)
    reach = max(1, E)
    for off in range(-reach, reach + 1):
        row = r + off
        ok = (row >= 0) & (row < R)
        for k in range(C):
            if off == 0 and k == 0:
                continue
            col = lax.rem(c + k, C)

            @pl.when(ok)
            def _():
                greet(dev(row, col))

            count = count + jnp.where(ok, 1, 0)

    for i in range(len(loads)):
        load(i).start()
    for i in range(1, 4):
        load(i).wait()
    for m in range(members):
        fc[grp, m] = base[...] + dot(dect[...], hid[m], NT)
    load(0).wait()
    pl.semaphore_wait(barrier, count)

    half = rows // PIECES

    def q_copy(m, q, up, piece):
        ref = q_buf.at[m, q, pl.ds(piece * half, half)]
        return remote(
            ref, ref, q_snd.at[m, up, q, piece], q_rcv.at[m, q, piece], dev(r + (1 if up else -1), c)
        )

    def c_copy(q, up, kind):
        ref = (cols, terms)[kind]
        return remote(
            ref.at[q], ref.at[q], c_snd.at[kind, up, q], c_rcv.at[kind, q], dev(r + (1 if up else -1), c)
        )

    def passes(up, h):
        if up:
            return r - h, (r - h >= 0) & (r + 1 < R)
        return r + h, (r + h < R) & (r - 1 >= 0)

    def send_q(m, h, pieces):
        for piece in pieces:
            for up in (1, 0):
                q, ok = passes(up, h)

                @pl.when(ok)
                def _():
                    if h > 0:
                        q_copy(m, q, up, piece).wait_recv()
                    q_copy(m, q, up, piece).start()

    def send_c(h):
        for up in (1, 0):
            q, ok = passes(up, h)

            @pl.when(ok)
            def _():
                for kind in range(2):
                    if h > 0:
                        c_copy(q, up, kind).wait_recv()
                    c_copy(q, up, kind).start()

    def host_of(s):
        q = lax.div(s, C)
        col = lax.rem(s, C)
        far = jnp.abs(q - r) > D
        row = jnp.where(far, jnp.where(q > r, q - D, q + D), r)
        slot = jnp.where(far, R * C + (jnp.abs(row - r) - 1) * C + c, q * C + c)
        return row, col, slot, far

    def kv_copy(m, s):
        row, col, slot, _ = host_of(s)
        return remote(
            pick_buf.at[m, s], kv_buf.at[m, slot], kv_snd.at[m, s], kv_rcv.at[m, slot], dev(row, col)
        )

    def send_near(m):
        def one(i, carry):
            dist = lax.div(i + 1, 2)
            q = jnp.where(lax.rem(i, 2) == 0, r + dist, r - dist)
            ok = (q >= 0) & (q < R)
            for k in range(1, C):

                @pl.when(ok)
                def _():
                    kv_copy(m, q * C + lax.rem(c + k, C)).start()

            return carry

        lax.fori_loop(0, 2 * D + 1, one, 0)

    def send_far(m, straight):
        def one(q, carry):
            @pl.when(jnp.abs(q - r) > D)
            def _():
                for k in range(0, 1) if straight else range(1, C):
                    kv_copy(m, q * C + lax.rem(c + k, C)).start()

            return carry

        if E > 0:
            lax.fori_loop(0, R, one, 0)

    def f_copy(src, sem, to):
        return remote(fc.at[src], fc.at[src], f_snd.at[sem], f_rcv.at[src], {"member": to})

    send_q(0, 0, range(PIECES))
    for k in cousins:
        f_copy(grp, k, lax.rem(grp + 2 * k, groups)).start()
    f_copy(grp, 0, mate).start()
    load(4).wait()
    load(5).wait()

    def pick(i, carry):
        m = lax.div(i, n)
        s = lax.rem(i, n)
        block = listed_block(me, owner_ref, local_ref, s)
        row, col, slot, _ = host_of(s)
        mine = (row == r) & (col == c)
        key = k_vm[m, block]
        value = v_vm[m, block]

        @pl.when(mine)
        def _():
            kv_buf[m, slot, 0] = key
            kv_buf[m, slot, 1] = value

        @pl.when(jnp.logical_not(mine))
        def _():
            pick_buf[m, s, 0] = key
            pick_buf[m, s, 1] = value

        return carry

    lax.fori_loop(0, members * n, pick, 0)
    for i in range(6, len(loads)):
        load(i).wait()
    select[...] = (
        lax.broadcasted_iota(jnp.int32, (rows, rows), 0) == order[...]
    ).astype(jnp.bfloat16)
    send_near(0)
    send_far(0, True)
    for m in range(members):
        dqs[m, 0, 0] = dot(hid[m], select[...], TN).astype(jnp.bfloat16)
        terms[r, m, pl.ds(0, heads)] = lse[m]

    for h in range(1, D):
        send_q(0, h, range(1))
    for k in cousins:
        src = lax.rem(grp + 2 * k, groups)
        f_copy(src, 0, mate).wait_recv()
        f_copy(src, groups // 2 + k, mate).start()
    for k in range(groups // 2):
        f_copy(lax.rem(mate + 2 * k, groups), 0, mate).wait_recv()

    everyone = members * groups
    lanes_step = 128

    def score(i, carry):
        lanes = pl.ds(pl.multiple_of(i * lanes_step, lanes_step), lanes_step)
        weight = LOSS_SCALE * share[:, lanes]
        for m in range(members):
            own = fc[grp, m, :, lanes]
            couple = jnp.zeros_like(own)
            for other in range(groups):
                for k in range(members):
                    couple = couple + unit(own - fc[other, k, :, lanes])
            polarity = unit(own - truth[:, lanes])
            deriv[m, :, lanes] = (
                weight
                * (polarity / everyone - (1.0 - FAIR_EPS) / (everyone * (everyone - 1)) * couple)
            ).astype(jnp.bfloat16)
        return carry

    lax.fori_loop(0, rows // lanes_step, score, 0)

    def latent(column):
        grads[...] = dot(dect[...], column, TN).astype(jnp.bfloat16)

    for m in range(members):
        column = dot(deriv[m], select[...], NN).astype(jnp.bfloat16)
        cols[r, m] = column
        latent(column)
        for h in range(heads):
            span = pl.ds(h * dim, dim)
            terms[r, m, pl.ds(heads + h, 1)] = jnp.sum(
                grads[span].astype(jnp.float32) * dqs[m, 0, 0, span].astype(jnp.float32),
                axis=0,
                keepdims=True,
            )
    send_c(0)
    for h in range(1, D):
        send_q(0, h, range(1, PIECES))
    send_far(0, False)
    for m in range(1, members):
        send_near(m)

    low = lax.broadcasted_iota(jnp.int32, (kb, pair), 1) < dim

    def tile(m, q, slot):
        for p in range(heads // 2):
            lanes = pl.ds(p * pair, pair)
            key = kv_buf[m, slot, 0, :, lanes]
            value = kv_buf[m, slot, 1, :, lanes]
            nought = jnp.zeros_like(key)
            keys = jnp.concatenate(
                [jnp.where(low, key, nought), jnp.where(low, nought, key)], axis=0
            )
            values = jnp.concatenate(
                [jnp.where(low, value, nought), jnp.where(low, nought, value)], axis=0
            )
            q_pair = q_buf[m, q, :, lanes]
            g_pair = grads[lanes, :]
            scores = dot(keys, q_pair, NT)
            dprobs = dot(values, g_pair, NN)
            prob, dscore = [], []
            for k in range(2):
                span = slice(k * kb, (k + 1) * kb)
                h = 2 * p + k
                pr = jnp.exp(scores[span] * scale - terms[q, m, pl.ds(h, 1), :])
                prob.append(pr.astype(jnp.bfloat16))
                dscore.append(
                    (pr * (dprobs[span] - terms[q, m, pl.ds(heads + h, 1), :])).astype(jnp.bfloat16)
                )
            prob = jnp.concatenate(prob, axis=0)
            dscore = jnp.concatenate(dscore, axis=0)
            dv = dot(prob, g_pair, NT)
            dk = dot(dscore, q_pair, NN) * scale
            kvg[m, slot, 0, :, lanes] = jnp.where(low, dk[:kb], dk[kb:]).astype(jnp.bfloat16)
            kvg[m, slot, 1, :, lanes] = jnp.where(low, dv[:kb], dv[kb:]).astype(jnp.bfloat16)
            total[lanes, :] += dot(keys, dscore, TN)

    def tile_place(q, t):
        turn = lax.div(t, C)
        row = jnp.where(q > r, r - turn, r + turn)
        slot = jnp.where(turn == 0, q * C + t, R * C + t - C)
        return row, lax.rem(t, C), slot, t == c

    def tile_count(q):
        extra = jnp.where(q == r + D, r, jnp.where(q == r - D, R - 1 - r, 0))
        return C * (1 + extra)

    def g_copy(m, q, t):
        row, col, slot, _ = tile_place(q, t)
        return remote(
            kvg.at[m, slot],
            land.at[m, q * C + c],
            g_snd.at[m, slot],
            g_rcv.at[m, q * C + c],
            dev(row, col),
        )

    def kv_arrival(m, slot):
        return remote(
            pick_buf.at[0, 0], kv_buf.at[m, slot], kv_snd.at[0, 0], kv_rcv.at[m, slot], dev(r, c)
        )

    def d_copy(m, dist, side, last):
        src, snd = dqs.at[m, dist - 1, side], d_snd.at[m, dist - 1, side]
        device = dev(r + 1 - 2 * side, c)
        if last:
            return remote(src, dq_in.at[m, side], snd, l_rcv.at[m, side], device)
        return remote(src, dqr.at[m, dist - 2, side], snd, d_rcv.at[m, dist - 2, side], device)

    plan = [(0, 0)] + [(0, d) for d in range(1, D)]
    plan += [(m, 0) for m in range(1, members)] + [(0, D)]
    relay_at = len(plan)
    for m in range(1, members):
        plan += [(m, d) for d in range(1, D + 1)]

    def table(step, values):
        found = jnp.int32(values[0])
        for k, value in enumerate(values):
            found = jnp.where(step == k, jnp.int32(value), found)
        return found

    def job(i, carry):
        step = lax.div(i, 2)
        side = lax.rem(i, 2)
        m = table(step, [a for a, _ in plan])
        dist = table(step, [b for _, b in plan])
        q = r + dist - 2 * dist * side
        ok = (q >= 0) & (q < R) & ((dist > 0) | (side == 0))

        @pl.when(i == 2)
        def _():
            for h in range(1, D):
                send_c(h)
            for k in range(1, members):
                send_q(k, 0, range(PIECES))
            for k in range(1, members):
                send_far(k, True)
                send_far(k, False)

        @pl.when(i == 2 * relay_at)
        def _():
            for k in range(1, members):
                for h in range(1, D):
                    send_q(k, h, range(PIECES))
            for far_side in range(2):
                far_q = r + D - 2 * D * far_side

                @pl.when((far_q >= 0) & (far_q < R))
                def _():
                    d_copy(0, D, far_side, D == 1).start()

                    def late(t, carry):
                        g_copy(0, far_q, t).start()
                        return carry

                    lax.fori_loop(C, tile_count(far_q), late, 0)

        @pl.when(ok)
        def _():
            for up in (1, 0):
                edge = (r == R - 1) if up else (r == 0)
                here = ((q < r) if up else (q > r)) & ((dist == D) | edge)

                @pl.when(here)
                def _():
                    for piece in range(PIECES):
                        q_copy(m, q, up, piece).wait_recv()

                    @pl.when(m == 0)
                    def _():
                        c_copy(q, up, 0).wait_recv()
                        c_copy(q, up, 1).wait_recv()

            latent(cols[q, m])
            total[...] = jnp.zeros_like(total)

            def one(t, carry):
                _, _, slot, mine = tile_place(q, t)

                @pl.when(jnp.logical_not(mine))
                def _():
                    kv_arrival(m, slot).wait_recv()

                tile(m, q, slot)

                @pl.when(jnp.logical_not(mine) & ((t < C) | (m > 0)))
                def _():
                    g_copy(m, q, t).start()

                return carry

            lax.fori_loop(0, tile_count(q), one, 0)

            @pl.when(dist == 0)
            def _():
                acc[m] = total[...] * scale

            @pl.when((dist > 0) & (dist < D))
            def _():
                part[m, jnp.minimum(jnp.maximum(dist - 1, 0), max(D - 2, 0)), side] = total[...] * scale

            @pl.when(dist == D)
            def _():
                dqs[m, D - 1, side] = (total[...] * scale).astype(jnp.bfloat16)

                @pl.when(m > 0)
                def _():
                    d_copy(m, D, side, D == 1).start()

        return carry

    lax.fori_loop(0, 2 * len(plan), job, 0)

    for m in range(members):
        for dist in range(D - 1, 0, -1):
            for side in range(2):
                q = r + dist - 2 * dist * side
                chained = (r > 0) if side == 0 else (r < R - 1)
                ok = (q >= 0) & (q < R)

                @pl.when(ok & chained)
                def _():
                    d_copy(m, dist + 1, side, False).wait_recv()
                    dqs[m, dist - 1, side] = (
                        part[m, dist - 1, side] + dqr[m, dist - 1, side].astype(jnp.float32)
                    ).astype(jnp.bfloat16)

                @pl.when(ok & jnp.logical_not(chained))
                def _():
                    dqs[m, dist - 1, side] = part[m, dist - 1, side].astype(jnp.bfloat16)

                @pl.when(ok)
                def _():
                    d_copy(m, dist, side, dist == 1).start()

    def kv_out(m, kind):
        return pltpu.make_async_copy(kv_sum.at[m, kind], (gk_out, gv_out)[kind].at[m], o_sem.at[m, kind])

    def q_out(m):
        return pltpu.make_async_copy(dq_sum.at[m], gq_out.at[m], o_sem.at[m, 2])

    def landed(ref, m, s, col, row):
        return remote(kvg.at[0, 0], ref, g_snd.at[0, 0], g_rcv.at[m, s], dev(row, col))

    chunk = 32

    def gather(m):
        kv_sum[m] = jnp.zeros_like(kv_sum[m])

        def one(i, carry):
            dist = lax.div(i, 2 * C)
            side = lax.rem(lax.div(i, C), 2)
            q = r + dist - 2 * dist * side
            ok = (q >= 0) & (q < R) & ((dist > 0) | (side == 0))

            @pl.when(ok)
            def _():
                s = q * C + lax.rem(i, C)
                row, col, slot, _ = host_of(s)
                mine = (row == r) & (col == c)
                block = listed_block(me, owner_ref, local_ref, s)

                def add(ref, a, b):
                    def rows_of(j, carry):
                        span = pl.ds(pl.multiple_of(j * chunk, chunk), chunk)
                        for kind in range(2):
                            value = ref[a, b, kind, span].astype(jnp.float32)
                            for k in range(kv_sum.shape[2]):
                                kv_sum[m, kind, k, span] += jnp.where(block == k, value, 0.0)
                        return carry

                    lax.fori_loop(0, kb // chunk, rows_of, 0)

                @pl.when(mine)
                def _():
                    add(kvg, m, slot)

                @pl.when(jnp.logical_not(mine))
                def _():
                    landed(land.at[m, s], m, s, col, row).wait_recv()
                    if near:
                        add(land, m, s)
                    else:
                        bring = pltpu.make_async_copy(land.at[m, s], stage.at[0, 0], ld_sem.at[0])
                        bring.start()
                        bring.wait()
                        add(stage, 0, 0)

            return carry

        lax.fori_loop(0, 2 * C * R, one, 0)
        for kind in range(2):
            kv_out(m, kind).start()

    for m in range(members):
        gather(m)
    for m in range(members):
        for side in range(2):
            @pl.when((r > 0) if side == 0 else (r < R - 1))
            def _():
                d_copy(m, 1, side, True).wait_recv()
                acc[m] = acc[m] + dq_in[m, side].astype(jnp.float32)
        dq_sum[m] = acc[m].T
        q_out(m).start()

    def last(i, carry):
        m = lax.div(i, n)
        s = lax.rem(i, n)
        row, col, _, _ = host_of(s)

        @pl.when((row != r) | (col != c))
        def _():
            kv_copy(m, s).wait_send()

        return carry

    lax.fori_loop(0, members * n, last, 0)

    def sent(i, carry):
        m = lax.div(i, R)
        q = lax.rem(i, R)

        @pl.when(jnp.abs(q - r) <= D)
        def _():
            def one(t, carry):
                @pl.when(jnp.logical_not(tile_place(q, t)[3]))
                def _():
                    g_copy(m, q, t).wait_send()

                return carry

            lax.fori_loop(0, tile_count(q), one, 0)

        return carry

    lax.fori_loop(0, members * R, sent, 0)
    for m in range(members):
        for dist in range(1, D + 1):
            for side in range(2):
                q = r + dist - 2 * dist * side

                @pl.when((q >= 0) & (q < R))
                def _():
                    d_copy(m, dist, side, dist == 1).wait_send()

    for h in range(D):
        for up in (1, 0):
            q, ok = passes(up, h)

            @pl.when(ok)
            def _():
                for m in range(members):
                    for piece in range(PIECES):
                        q_copy(m, q, up, piece).wait_send()
                for kind in range(2):
                    c_copy(q, up, kind).wait_send()

    f_copy(grp, 0, mate).wait_send()
    for k in cousins:
        f_copy(grp, k, mate).wait_send()
        f_copy(grp, groups // 2 + k, mate).wait_send()
    for m in range(members):
        for kind in range(2):
            kv_out(m, kind).wait()
        q_out(m).wait()


def fused(groups, n, heads, blocks, arrays):
    (_, _, hid, dect, base, truth, share, order, q, k, v, lse) = arrays
    C = columns_of(n)
    R = n // C
    D = R // 2
    E = R - 1 - D
    members, rows, width = hid.shape
    chans = base.shape[0]
    bf, f32 = jnp.bfloat16, jnp.float32
    slots = (R + E) * C
    vm = pltpu.VMEM
    dma = pltpu.SemaphoreType.DMA
    scratch = [
        vm(hid.shape, bf),
        vm(dect.shape, bf),
        vm(base.shape, f32),
        vm(truth.shape, f32),
        vm(share.shape, f32),
        vm(order.shape, jnp.int32),
        vm(lse.shape, f32),
        vm(k.shape, bf),
        vm(v.shape, bf),
        vm((groups, members, chans, rows), f32),
        vm((rows, rows), bf),
        vm((members, chans, rows), bf),
        vm((R, members, chans, rows), bf),
        vm((R, members, 2 * heads, rows), f32),
        vm((members, R, rows, width), bf),
        vm((members, n, 2, KB, width), bf),
        vm((members, slots, 2, KB, width), bf),
        vm((members, slots, 2, KB, width), bf),
        vm((members, 2, blocks, KB, width), f32),
        vm((members, rows, width), f32),
        vm((members, width, rows), f32),
        vm((members, max(D - 1, 1), 2, width, rows), f32),
        vm((members, D, 2, width, rows), bf),
        vm((members, max(D - 1, 1), 2, width, rows), bf),
        vm((members, 2, width, rows), bf),
        vm((width, rows), bf),
        vm((width, rows), f32),
        dma((10,)),
        dma((groups,)),
        dma((groups,)),
        dma((members, 2, R, PIECES)),
        dma((members, R, PIECES)),
        dma((2, 2, R)),
        dma((2, R)),
        dma((members, n)),
        dma((members, slots)),
        dma((members, slots)),
        dma((members, n)),
        dma((members, D, 2)),
        dma((members, max(D - 1, 1), 2)),
        dma((members, 2)),
        dma((members, 3)),
    ]
    sums = [(members, rows, width)] + 2 * [(members, blocks, KB, width)]
    held = sum(
        math.prod(x.shape) * jnp.dtype(x.dtype).itemsize
        for x in scratch
        if getattr(x, "memory_space", None) == pltpu.VMEM
    )
    out_bytes = sum(4 * math.prod(x) for x in sums)
    land = (members, n, 2, KB, width)
    near = held + out_bytes + 2 * math.prod(land) + VMEM_SPARE <= VMEM_LIMIT
    if near:
        scratch = [vm(land, bf)] + scratch + [vm((8, 128), bf)]
    else:
        scratch = scratch + [vm((1, 1) + land[2:], bf)]
    limit = VMEM_LIMIT - out_bytes - VMEM_GAP if near else VMEM_LIMIT
    out_type = pltpu.VMEM if near else jax.ShapeDtypeStruct
    smem = pl.BlockSpec(memory_space=pltpu.SMEM)
    anyw = pl.BlockSpec(memory_space=pl.ANY)
    tiles = members * n
    return pl.pallas_call(
        functools.partial(fused_kernel, groups, C, R, heads, near),
        out_shape=[out_type(x, f32) for x in sums]
        + ([] if near else [jax.ShapeDtypeStruct(land, bf)]),
        in_specs=[smem, smem] + [anyw] * 10,
        out_specs=[anyw] * (3 if near else 4),
        scratch_shapes=scratch,
        compiler_params=pltpu.CompilerParams(
            collective_id=0, has_side_effects=True, vmem_limit_bytes=limit
        ),
        cost_estimate=pl.CostEstimate(
            flops=tiles * 10 * rows * KB * width,
            bytes_accessed=16 * 2**20,
            transcendentals=tiles * heads * rows * KB,
        ),
        name="fused",
    )(*arrays), not near


def finish_kernel(staged, *refs):
    arrays = (len(refs) - 2) // (3 if staged else 2)
    stages, read, write = refs[2 * arrays : -2], refs[-2], refs[-1]
    pieces = [(k, m) for m in range(refs[0].shape[0]) for k in range(arrays)]

    def get(k, m):
        return pltpu.make_async_copy(refs[k].at[m], stages[k].at[m], read.at[k, m])

    def put(k, m):
        src = stages[k] if staged else refs[k]
        return pltpu.make_async_copy(src.at[m], refs[arrays + k].at[m], write.at[k, m])

    if staged:
        for piece in pieces:
            get(*piece).start()
    for piece in pieces:
        if staged:
            get(*piece).wait()
        put(*piece).start()
    for piece in pieces:
        put(*piece).wait()


def finish(arrays, staged):
    anyw = pl.BlockSpec(memory_space=pl.ANY)
    sems = pltpu.SemaphoreType.DMA((len(arrays), arrays[0].shape[0]))
    stages = [pltpu.VMEM(x.shape, x.dtype) for x in arrays] if staged else []
    return pl.pallas_call(
        functools.partial(finish_kernel, staged),
        out_shape=[jax.ShapeDtypeStruct(x.shape, x.dtype) for x in arrays],
        in_specs=[anyw] * len(arrays),
        out_specs=[anyw] * len(arrays),
        scratch_shapes=stages + [sems, sems],
        compiler_params=pltpu.CompilerParams(vmem_limit_bytes=(48 if staged else 1) * 2**20),
        cost_estimate=pl.CostEstimate(flops=10**6, bytes_accessed=12 * 2**20, transcendentals=0),
        name="finish",
    )(*arrays)


def shards(
    groups,
    n,
    hidden_embedding,
    decoder_matrix,
    baseline_field,
    truth_field,
    cell_surface_share,
    node_order,
    query,
    key_rows,
    value_rows,
    row_lse,
    kv_owner,
    kv_local,
):
    members, nodes, width = hidden_embedding.shape
    heads = row_lse.shape[1]
    blocks = nodes // KB
    split = (members, blocks, KB, width)
    out, staged = fused(
        groups,
        n,
        heads,
        blocks,
        (
            kv_owner,
            kv_local,
            hidden_embedding,
            decoder_matrix.T,
            baseline_field,
            truth_field,
            cell_surface_share[None],
            node_order,
            query,
            key_rows.reshape(split),
            value_rows.reshape(split),
            row_lse,
        ),
    )
    gq, gk, gv = finish(out[:3], staged)
    return gq, gk.reshape(key_rows.shape), gv.reshape(value_rows.shape)


def solution(mesh):
    rows = P("member", "mesh", None)
    return jax.shard_map(
        functools.partial(shards, mesh.shape["member"], mesh.shape["mesh"]),
        mesh=mesh,
        in_specs=(
            rows,
            P(),
            P(None, "mesh"),
            P(None, "mesh"),
            P("mesh"),
            P("mesh", None),
            rows,
            rows,
            rows,
            P("member", None, "mesh"),
            P(),
            P(),
        ),
        out_specs=(rows, rows, rows),
        check_vma=False,
    )
```

time: 144 us -> 115 us (0.80)
  Pallas kernels: 137 us -> 113 us
  local copies, waits for them, and re-layouts: 5.43 us -> 0 us
    pallas_call x2, Pallas kernels: 137 us -> 113 us  [the longest x1 111 us: fused(): pl.pallas_call(functools.partial(fused_kernel, groups, C, R, heads, near)...]
    unnamed x9 -> x0, local copies, waits for them, and re-layouts: 5.43 us -> none
where the time goes in v1:
time: 115 us; the launch traced here: 114 us
  Pallas kernels  113 us (98%)
    pallas_call x1, Pallas kernels, fused(): pl.pallas_call(functools.partial(fused_kernel, groups, C, R, heads, near)...  111 us
    pallas_call x1, Pallas kernels, finish(): pl.pallas_call(functools.partial(finish_kernel, staged), out_shape=[jax.S...  2.78 us

profile of v1, /device:TPU:10, one launch (start us, length us, event | category | flops | bytes accessed | tf_op | source)
XLA Modules:
  0.0 114.1 jit_solution(7830496899118520333)
XLA Ops:
  0.6 110.7 %fused.1 = (f32[2,512,512]{2,1,0:T(8,128)S(1)}, f32[2,4,128,512]{3,2,1,0:T(8,128)S(1)}, f32[2,4,128,512]{3,2,1,0:T(8,128)S(1)}) custom-call(s32[8,8]{1,0:T(8,128)} %owner_ref.1, s32[8,8]{1,0:T(8,128)} %local_ref.1, bf16[2,512,512]{2,1,0:T(8,128)(2,1)} %hid_in.1, bf16[96,512]{1,0:T(8,128)(2,1)} %bitcast.10, f32[96,512]{1,0:T(8,128)} %base_in.1, ...), custom_call_target="tpu_custom_call" | custom-call | flops 5368709120 | bytes 16777216 | tf_op jit(solution)/shard_map/fused/pallas_call | solution.py:764
  111.4 2.8 %finish.1 = (f32[2,512,512]{2,1,0:T(8,128)}, f32[2,4,128,512]{3,2,1,0:T(8,128)}, f32[2,4,128,512]{3,2,1,0:T(8,128)}) custom-call(f32[2,512,512]{2,1,0:T(8,128)S(1)} %get-tuple-element.9.refs_0_, f32[2,4,128,512]{3,2,1,0:T(8,128)S(1)} %get-tuple-element.10.refs_1_, f32[2,4,128,512]{3,2,1,0:T(8,128)S(1)} %get-tuple-element.11.refs_2_), custom_call_target="tpu_custom_call" | custom-call | flops 1000000 | bytes 12582912 | tf_op jit(solution)/shard_map/finish/pallas_call | solution.py:810

commit v2 on v1

--- a/solution.py
+++ b/solution.py
@@ -136,11 +136,11 @@
 
     loads = [
         (q_in, None),
+        (k_in, k_vm),
+        (v_in, v_vm),
         (hid_in, hid),
         (dect_in, dect),
         (base_in, base),
-        (k_in, k_vm),
-        (v_in, v_vm),
         (order_in, order),
         (truth_in, truth),
         (share_in, share),
@@ -179,12 +179,6 @@
 
     for i in range(len(loads)):
         load(i).start()
-    for i in range(1, 4):
-        load(i).wait()
-    for m in range(members):
-        fc[grp, m] = base[...] + dot(dect[...], hid[m], NT)
-    load(0).wait()
-    pl.semaphore_wait(barrier, count)
 
     half = rows // PIECES
 
@@ -270,13 +264,6 @@
 
     def f_copy(src, sem, to):
         return remote(fc.at[src], fc.at[src], f_snd.at[sem], f_rcv.at[src], {"member": to})
-
-    send_q(0, 0, range(PIECES))
-    for k in cousins:
-        f_copy(grp, k, lax.rem(grp + 2 * k, groups)).start()
-    f_copy(grp, 0, mate).start()
-    load(4).wait()
-    load(5).wait()
 
     def pick(i, carry):
         m = lax.div(i, n)
@@ -299,14 +286,27 @@
 
         return carry
 
-    lax.fori_loop(0, members * n, pick, 0)
+    for i in range(1, 3):
+        load(i).wait()
+    lax.fori_loop(0, n, pick, 0)
+    load(0).wait()
+    pl.semaphore_wait(barrier, count)
+    send_q(0, 0, range(PIECES))
+    send_near(0)
+    for i in range(3, 6):
+        load(i).wait()
+    for m in range(members):
+        fc[grp, m] = base[...] + dot(dect[...], hid[m], NT)
+    for k in cousins:
+        f_copy(grp, k, lax.rem(grp + 2 * k, groups)).start()
+    f_copy(grp, 0, mate).start()
+    send_far(0, True)
+    lax.fori_loop(n, members * n, pick, 0)
     for i in range(6, len(loads)):
         load(i).wait()
     select[...] = (
         lax.broadcasted_iota(jnp.int32, (rows, rows), 0) == order[...]
     ).astype(jnp.bfloat16)
-    send_near(0)
-    send_far(0, True)
     for m in range(members):
         dqs[m, 0, 0] = dot(hid[m], select[...], TN).astype(jnp.bfloat16)
         terms[r, m, pl.ds(0, heads)] = lse[m]
@@ -459,11 +459,17 @@
                 send_far(k, True)
                 send_far(k, False)
 
+        @pl.when(i == 2 * (relay_at - 1))
+        def _():
+            for k in range(1, 2):
+                for h in range(1, min(D, 2)):
+                    send_q(k, h, range(1))
+
         @pl.when(i == 2 * relay_at)
         def _():
             for k in range(1, members):
                 for h in range(1, D):
-                    send_q(k, h, range(PIECES))
+                    send_q(k, h, range(1 if k == 1 and h == 1 else 0, PIECES))
             for far_side in range(2):
                 far_q = r + D - 2 * D * far_side
 
@@ -614,9 +620,7 @@
         for kind in range(2):
             kv_out(m, kind).start()
 
-    for m in range(members):
-        gather(m)
-    for m in range(members):
+    def settle(m):
         for side in range(2):
             @pl.when((r > 0) if side == 0 else (r < R - 1))
             def _():
@@ -625,6 +629,9 @@
         dq_sum[m] = acc[m].T
         q_out(m).start()
 
+    for m in range(members - 1):
+        gather(m)
+        settle(m)
     def last(i, carry):
         m = lax.div(i, n)
         s = lax.rem(i, n)
@@ -637,6 +644,8 @@
         return carry
 
     lax.fori_loop(0, members * n, last, 0)
+    gather(members - 1)
+    settle(members - 1)
 
     def sent(i, carry):
         m = lax.div(i, R)

time: 115 us -> 114 us (level)
    pallas_call x1, Pallas kernels: 111 us -> 109 us  [fused(): pl.pallas_call(functools.partial(fused_kernel, groups, C, R, heads, near)...]
where the time goes in v2:
time: 114 us; the launch traced here: 113 us
  Pallas kernels  112 us (98%)
    pallas_call x1, Pallas kernels, fused(): pl.pallas_call(functools.partial(fused_kernel, groups, C, R, heads, near)...  109 us
    pallas_call x1, Pallas kernels, finish(): pl.pallas_call(functools.partial(finish_kernel, staged), out_shape=[jax.S...  2.78 us

profile of v2, /device:TPU:10, one launch (start us, length us, event | category | flops | bytes accessed | tf_op | source)
XLA Modules:
  0.0 112.6 jit_solution(12530265658321546126)
XLA Ops:
  0.6 109.1 %fused.1 = (f32[2,512,512]{2,1,0:T(8,128)S(1)}, f32[2,4,128,512]{3,2,1,0:T(8,128)S(1)}, f32[2,4,128,512]{3,2,1,0:T(8,128)S(1)}) custom-call(s32[8,8]{1,0:T(8,128)} %owner_ref.1, s32[8,8]{1,0:T(8,128)} %local_ref.1, bf16[2,512,512]{2,1,0:T(8,128)(2,1)} %hid_in.1, bf16[96,512]{1,0:T(8,128)(2,1)} %bitcast.10, f32[96,512]{1,0:T(8,128)} %base_in.1, ...), custom_call_target="tpu_custom_call" | custom-call | flops 5368709120 | bytes 16777216 | tf_op jit(solution)/shard_map/fused/pallas_call | solution.py:773
  109.8 2.8 %finish.1 = (f32[2,512,512]{2,1,0:T(8,128)}, f32[2,4,128,512]{3,2,1,0:T(8,128)}, f32[2,4,128,512]{3,2,1,0:T(8,128)}) custom-call(f32[2,512,512]{2,1,0:T(8,128)S(1)} %get-tuple-element.9.refs_0_, f32[2,4,128,512]{3,2,1,0:T(8,128)S(1)} %get-tuple-element.10.refs_1_, f32[2,4,128,512]{3,2,1,0:T(8,128)S(1)} %get-tuple-element.11.refs_2_), custom_call_target="tpu_custom_call" | custom-call | flops 1000000 | bytes 12582912 | tf_op jit(solution)/shard_map/finish/pallas_call | solution.py:819
